TPU v7x, 32 devices: a whole 2x2x4 slice. The times are simulated.
32 devices in a mesh: grp: 2 (over x), tile: 4 (over z), mem: 4 (over y, core).
Axes of the slice: x: 2, y: 2, z: 4, core: 2. Of those that a mesh axis runs over, the one named last changes fastest.
Arguments:
- current_state: float32 [512, 2, 8192], P(('grp', 'mem'), None, 'tile'), may hold values from -6 to 6
- lagged_states: float32 [3, 4, 8, 512, 512], P(None, 'tile', ('grp', 'mem')), may hold values from -6 to 6
- water_depth: float32 [8192], P('tile'), may hold values from 0.4 to 1
- obs_cells: int32 [4096], replicated, may hold values from 0 to 8191, as said below
- obs_values: float32 [4096], replicated, may hold values from -6 to 6
- obs_errors: float32 [4096], replicated, may hold values from 0.5 to 2
- tile_obs: int32 [4, 8, 1024], P('tile', ('grp', 'mem')), may hold values from -1 to 4095, as said below
Outputs:
- analysis_state: float32 [512, 2, 8192], P(('grp', 'mem'), None, 'tile')
- smoothed_lags: float32 [3, 4, 8, 512, 512], P(None, 'tile', ('grp', 'mem'))
Inputs may be any that keep to these rules, and one draw needn't show every extreme that they name: `obs_cells`: observation o lies in grid tile o // 1024, that is at a cell from (o // 1024) * 2048 to that plus 2048 - 1. `tile_obs`: each list holds distinct indices of observations in its own grid tile or the two beside it (periodically), used slots first and -1 after them; at least 256 slots are used in every list, all 1024 in some list.
All inputs are finite; a program needn't handle non-finite values. Where the computation divides by a largest or mean magnitude, that divisor is 1e-20 or more.
Results may differ from a plain program's by a relative error of at most 0.0003.
Values sent between devices are 32-bit elements; how exact they have to be, the bound alone decides.
A program may use at most 64 MiB of HBM per device.

v0:
```python
import math

import jax
import jax.numpy as jnp
from jax import lax
from jax.sharding import PartitionSpec as P

OBS_DEV = 1024
ITERS = 6
MODEL_STEPS = 2
LOC = 512


flux_scale = 0.9
wave_scale = 0.9
highest = lax.Precision.HIGHEST


def shifted(array, axis, by):
    peers = lax.axis_size(axis)
    return lax.ppermute(array, axis, [(i, (i + by) % peers) for i in range(peers)])


def with_halo(block, sides, width):
    for axis, dim in sides:
        count = lax.axis_size(axis)
        forward = [(i, i + 1) for i in range(count - 1)]
        forward.append((count - 1, 0))
        backward = [(target, source) for source, target in forward]
        low = lax.ppermute(
            lax.slice_in_dim(block, block.shape[dim] - width, None, axis=dim), axis, forward
        )
        high = lax.ppermute(lax.slice_in_dim(block, 0, width, axis=dim), axis, backward)
        block = jnp.concatenate([low, block, high], axis=dim)
    return block


def advance(free_elevation, fluid_speed, water_depth):
    for repeat in range(MODEL_STEPS):
        velocity_left = shifted(fluid_speed[:, -1], "tile", 1)
        previous = jnp.concatenate([velocity_left[:, None], fluid_speed[:, :-1]], axis=1)
        free_elevation = free_elevation - flux_scale * water_depth * (fluid_speed - previous)
        height_right = shifted(free_elevation[:, 0], "tile", -1)
        following = jnp.concatenate([free_elevation[:, 1:], height_right[:, None]], axis=1)
        fluid_speed = fluid_speed - wave_scale * (following - free_elevation)
    return (free_elevation, fluid_speed)


def inverse_root(matrix, members):
    row_bound = jnp.max(jnp.sum(jnp.abs(matrix), axis=1))
    identity = jnp.eye(members, dtype=jnp.float32)

    def newton_step(repeat, carry):
        approx, root_inv = carry
        middle = 1.5 * identity - 0.5 * jnp.dot(root_inv, approx, precision=highest)
        return (
            jnp.dot(approx, middle, precision=highest),
            jnp.dot(middle, root_inv, precision=highest),
        )

    approx, root_inv = lax.fori_loop(0, ITERS, newton_step, (matrix / row_bound, identity))
    return root_inv / jnp.sqrt(row_bound)


def apply_transform(transform, states):
    state_mean = jnp.mean(states, axis=-2, keepdims=True)
    moved = jnp.einsum("ij,...iv->...jv", transform, states - state_mean, precision=highest)
    return state_mean + moved


def analyse_rows(
    patch_field_slab,
    lag_block,
    predicted_rows,
    obs_level,
    obs_spread,
    obs_sites,
    usable,
    center,
    cell_total,
):
    members = predicted_rows.shape[1]
    mean_obs = jnp.mean(predicted_rows, axis=1)
    spread_rows = predicted_rows - mean_obs[:, None]
    departure = obs_level - mean_obs
    distance = jnp.abs(obs_sites - center)
    distance = jnp.minimum(distance, cell_total - distance).astype(jnp.float32)
    weight = jnp.exp(-0.5 * (distance / LOC) ** 2) / (obs_spread * obs_spread)
    weight = jnp.where(usable, weight, jnp.zeros_like(weight))
    identity = jnp.eye(members, dtype=jnp.float32)
    weighted_rows = spread_rows * weight[:, None]
    product = lax.dot_general(
        weighted_rows, spread_rows, (((0,), (0,)), ((), ())), precision=highest
    )
    precision_matrix = (members - 1) * identity + product
    root_cover = inverse_root(precision_matrix, members)
    covariance = jnp.dot(root_cover, root_cover, precision=highest)
    innovation = jnp.dot(weight * departure, spread_rows, precision=highest)
    mean_weight = jnp.dot(covariance, innovation, precision=highest)
    transform = math.sqrt(members - 1) * root_cover + mean_weight[:, None]
    return (apply_transform(transform, patch_field_slab), apply_transform(transform, lag_block))


def per_device(
    current_state, lagged_states, water_depth, obs_cells, obs_values, obs_errors, tile_obs
):
    trial_slab_lines = current_state.shape[0]
    cells_dev = current_state.shape[2]
    group_size = lax.axis_size("grp")
    member_size = lax.axis_size("mem")
    trial_bundles = group_size * member_size
    tile_count = lax.axis_size("tile")
    tile_index = lax.axis_index("tile")
    part_index = lax.axis_index("grp") * member_size + lax.axis_index("mem")
    cell_total = cells_dev * tile_count
    obs_total = obs_values.shape[0]
    patch_point_number = cells_dev // trial_bundles
    members = trial_slab_lines * trial_bundles
    free_elevation, fluid_speed = advance(current_state[:, 0], current_state[:, 1], water_depth)
    prior_fields = jnp.stack([free_elevation, fluid_speed], axis=1)
    local_cells = (
        lax.dynamic_slice_in_dim(obs_cells, tile_index * OBS_DEV, OBS_DEV) - tile_index * cells_dev
    )
    obs_block = jnp.take(free_elevation.T, local_cells, axis=0, mode="clip")
    regrouped = lax.all_to_all(
        prior_fields.reshape(1, trial_slab_lines, 2, trial_bundles, patch_point_number),
        ("grp", "mem"),
        split_axis=3,
        concat_axis=0,
        tiled=True,
    )
    patch_field_slab = regrouped.reshape(members, 2 * patch_point_number)
    rows_here = tile_obs[0, 0]
    nearby = with_halo(obs_block, (("tile", 0),), OBS_DEV)
    row_lists = lax.all_gather(tile_obs, ("grp", "mem"), axis=1, tiled=True)[0]
    relative = (jnp.maximum(row_lists, 0) - (tile_index - 1) * OBS_DEV) % obs_total
    relative = jnp.where(row_lists >= 0, relative, 0)
    picked = jnp.take(nearby, relative.reshape(-1), axis=0, mode="clip")
    picked = picked.reshape(trial_bundles, rows_here.shape[0], trial_slab_lines)
    arrived = lax.all_to_all(picked, ("grp", "mem"), split_axis=0, concat_axis=2, tiled=True)
    predicted_rows = arrived.reshape(rows_here.shape[0], members)
    usable = rows_here >= 0
    clamped = jnp.maximum(rows_here, 0)
    center = tile_index * cells_dev + part_index * patch_point_number + patch_point_number // 2
    analysis, older = analyse_rows(
        patch_field_slab,
        lagged_states[:, 0, 0],
        predicted_rows,
        obs_values[clamped],
        obs_errors[clamped],
        obs_cells[clamped],
        usable,
        center,
        cell_total,
    )
    returned = lax.all_to_all(
        analysis.reshape(trial_bundles, trial_slab_lines, 2, 1, patch_point_number),
        ("grp", "mem"),
        split_axis=0,
        concat_axis=3,
        tiled=True,
    )
    analysis_state = returned.reshape(trial_slab_lines, 2, cells_dev)
    older_out = older[:, None, None]
    return (analysis_state, older_out)


def solution(mesh):
    placed = (
        P(("grp", "mem"), None, "tile"),
        P(None, "tile", ("grp", "mem"), None, None),
        P("tile"),
        P(),
        P(),
        P(),
        P("tile", ("grp", "mem"), None),
    )
    return jax.shard_map(
        per_device,
        mesh=mesh,
        in_specs=placed,
        out_specs=(P(("grp", "mem"), None, "tile"), P(None, "tile", ("grp", "mem"), None, None)),
        check_vma=False,
    )
```

profile of v0, /device:TPU:0, one launch (start us, length us, event | category | flops | bytes accessed | tf_op | source)
XLA Modules:
  0.0 192.8 jit_solution(15663174578931347264)
XLA Ops:
  0.6 3.4 %fusion.59 = (f32[64,1,2048]{2,1,0:T(1,128)}, f32[64,1,2048]{2,1,0:T(1,128)S(1)}) fusion(f32[64,2,2048]{2,1,0:T(2,128)} %param.9), kind=kLoop, calls=%fused_computation.113 | loop fusion | bytes 2097152 | tf_op jit(solution)/shard_map/slice | solution.py:119
  4.6 3.1 %collective-permute-start = (f32[64]{0:T(128)S(1)}, f32[64]{0:T(128)S(1)}, u32[]{:S(2)}, u32[]{:S(2)}) collective-permute-start(f32[64]{0:T(128)S(1)} %slice_bitcast_fusion.4), channel_id=1, source_target_pairs={{0,4},{4,8},{8,12},{12,0},{1,5},{5,9},{9,13},{13,1},{2,6},{6,10},{... | collective-permute-start | bytes 776 | tf_op jit(solution)/shard_map/ppermute | solution.py:21
  8.8 9.1 %all_gather.3 = s32[1,8,1024]{2,0,1:T(1,128)S(1)} all-gather(s32[1,1,1024]{2,0,1:T(1,128)S(1)} %bitcast.130), channel_id=1, replica_groups=mesh['grp'=2,'tile'=4,'mem'=4] {'grp','mem'}, dimensions={1}, use_global_device_ids=true | all-gather | bytes 36864 | tf_op jit(solution)/shard_map/all_gather | solution.py:135
  19.8 2.3 %collective-permute-start.1 = (f32[64]{0:T(128)S(1)}, f32[64]{0:T(128)S(1)}, u32[]{:S(2)}, u32[]{:S(2)}) collective-permute-start(f32[64]{0:T(128)S(1)} %slice_bitcast_fusion.3), channel_id=1, source_target_pairs={{0,12},{4,0},{8,4},{12,8},{1,13},{5,1},{9,5},{13,9},{2,14},{6,2},{... | collective-permute-start | bytes 776 | tf_op jit(solution)/shard_map/ppermute | solution.py:21
  23.7 1.6 collective-permute-start.2
  26.4 2.9 %collective-permute-done.2 = f32[64]{0:T(128)S(1)} collective-permute-done((f32[64]{0:T(128)S(1)}, f32[64]{0:T(128)S(1)}, u32[]{:S(2)}, u32[]{:S(2)}) %collective-permute-start.2) | collective-permute-done | bytes 288 | tf_op jit(solution)/shard_map/ppermute | solution.py:21
  29.7 2.1 %collective-permute-start.3 = (f32[64]{0:T(128)S(1)}, f32[64]{0:T(128)S(1)}, u32[]{:S(2)}, u32[]{:S(2)}) collective-permute-start(f32[64]{0:T(128)S(1)} %slice_bitcast_fusion.1), channel_id=1, source_target_pairs={{0,12},{4,0},{8,4},{12,8},{1,13},{5,1},{9,5},{13,9},{2,14},{6,2},{... | collective-permute-start | bytes 776 | tf_op jit(solution)/shard_map/ppermute | solution.py:21
  32.8 4.0 %gather_fusion = f32[1024,64]{1,0:T(8,128)} fusion(f32[2048,64]{1,0:T(8,128)S(1)} %bitcast.115, s32[1024]{0:T(1024)S(1)} %subtract_clamp_fusion), kind=kCustom, calls=%fused_computation | custom fusion | bytes 528384 | tf_op jit(solution)/shard_map/jit(_take)/gather | solution.py:124
  36.8 2.0 %collective-permute-start.4 = (f32[1024,64]{1,0:T(8,128)}, f32[1024,64]{1,0:T(8,128)}, u32[]{:S(2)}, u32[]{:S(2)}) collective-permute-start(f32[1024,64]{1,0:T(8,128)} %gather_fusion), channel_id=1, source_target_pairs={{0,4},{4,8},{8,12},{12,0},{1,5},{5,9},{9,13},{13,1},{2,6},{6,10},{... | collective-permute-start | bytes 786440 | tf_op jit(solution)/shard_map/ppermute | solution.py:30
  38.8 3.8 %fusion.18 = (f32[64,1,2048]{0,2,1:T(8,128)}, f32[64,1,2048]{0,2,1:T(8,128)S(1)}) fusion(f32[64,1,1]{0,2,1:T(1,128)S(1)} %bitcast.144, f32[64,1,2047]{0,2,1:T(8,128)} %slice_bitcast_fusion, f32[64,1,2048]{0,2,1:T(8,128)S(1)} %copy.52, f32[64,1,1]{0,2,1:T(1,128)S(1)} %bitcast.140, f32[64,1,2047]{0,2,1:T(8,128)} %get-tuple-element.69, ...), kind=kLoop, calls=%fused_computation.41 | loop fusion | flops 2097152 | bytes 4202496 | tf_op jit(solution)/shard_map/sub | solution.py:45
  44.7 1.9 pad_maximum_fusion.1
  46.6 3.6 %all-to-all-start = ((f32[1,64,2,8,256]{4,2,1,0,3:T(2,128)}), f32[1,64,2,8,256]{4,2,1,0,3:T(2,128)S(1)}, u32[]{:S(2)}, u32[]{:S(2)}) async-start(f32[1,64,2,8,256]{4,2,1,0,3:T(2,128)} %pad_maximum_fusion.1), calls=%async_computation | async-start | bytes 2097152 | tf_op jit(solution)/shard_map/all_to_all | solution.py:125
  50.3 9.6 %collective-permute-done.5 = f32[1024,64]{1,0:T(8,128)} collective-permute-done((f32[1024,64]{1,0:T(8,128)}, f32[1024,64]{1,0:T(8,128)}, u32[]{:S(2)}, u32[]{:S(2)}) %collective-permute-start.5) | collective-permute-done | bytes 262176 | tf_op jit(solution)/shard_map/ppermute | solution.py:33
  61.3 27.8 %gather_fusion.1 = f32[8192,64]{1,0:T(8,128)} fusion(f32[3072,64]{1,0:T(8,128)S(1)} %pad_maximum_fusion, s32[8192]{0:T(1024)S(1)} %broadcast_clamp_fusion), kind=kCustom, calls=%fused_computation.1 | custom fusion | bytes 4227072 | tf_op jit(solution)/shard_map/jit(_take)/gather | solution.py:138
  89.0 3.8 %copy.41 = f32[8,1024,64]{1,2,0:T(8,128)} copy(f32[8,1024,64]{2,1,0:T(8,128)} %bitcast.120) | data formatting | bytes 4194304 | tf_op jit(solution)/shard_map/reshape | solution.py:139
  93.8 3.8 %all-to-all-start.1 = ((f32[8,1024,64]{1,2,0:T(8,128)}), f32[8,1024,64]{1,2,0:T(8,128)S(1)}, u32[]{:S(2)}, u32[]{:S(2)}) async-start(f32[8,1024,64]{1,2,0:T(8,128)} %copy.41), calls=%async_computation.1 | async-start | bytes 4194304 | tf_op jit(solution)/shard_map/all_to_all | solution.py:140
  97.6 6.2 %gather_fusion.2 = s32[1024]{0:T(1024)S(1)} fusion(s32[4096]{0:T(1024)S(1)} %copy-done.1, s32[1024]{0:T(1024)S(1)} %broadcast_clamp_fusion.1), kind=kCustom, calls=%fused_computation.2 | custom fusion | bytes 12288 | tf_op jit(solution)/shard_map/gather | solution.py:151
  103.8 6.2 %gather_fusion.3 = f32[1024]{0:T(1024)S(1)} fusion(f32[4096]{0:T(1024)S(1)} %copy-done, s32[1024]{0:T(1024)S(1)} %broadcast_clamp_fusion.1), kind=kCustom, calls=%fused_computation.3 | custom fusion | bytes 12288 | tf_op jit(solution)/shard_map/gather | solution.py:150
  109.9 6.2 %gather_fusion.4 = f32[1024]{0:T(1024)S(1)} fusion(f32[4096]{0:T(1024)S(1)} %copy-done.2, s32[1024]{0:T(1024)S(1)} %broadcast_clamp_fusion.1), kind=kCustom, calls=%fused_computation.4 | custom fusion | bytes 12288 | tf_op jit(solution)/shard_map/gather | solution.py:149
  118.8 2.4 %copy.54 = f32[64,8,2,256]{3,1,2,0:T(8,128)} copy(f32[64,8,2,256]{3,2,1,0:T(2,128)} %bitcast.121) | data formatting | bytes 2097152
  123.7 3.6 %abs_reduce_fusion = (f32[512]{0:T(512)S(1)}, f32[512,512]{0,1:T(8,128)S(1)}) fusion(f32[1024,512]{0,1:T(8,128)S(1)} %bitcast.122, f32[1024,512]{0,1:T(8,128)S(1)} %bitcast.118), kind=kOutput, calls=%fused_computation.47 | convolution fusion | flops 3222535680 | bytes 5244928 | tf_op jit(solution)/shard_map/dot_general | solution.py:92
  129.4 34.7 %while.13 = (s32[]{:T(128)}, f32[512,512]{0,1:T(8,128)S(1)}, f32[512,512]{1,0:T(8,128)S(1)}, s32[]{:T(128)}) while((s32[]{:T(128)}, f32[512,512]{0,1:T(8,128)S(1)}, f32[512,512]{1,0:T(8,128)S(1)}, s32[]{:T(128)}) %tuple.43), condition=%wide.region_5.6_spmd.clone, body=%wide.region_4.5_spmd.clone.sunk | while | flops 4832886784 | bytes 13631541 | solution.py:61
  129.6 1.9 fusion.87
  131.4 1.8 convolution_bitcast_fusion.3
  133.3 1.8 fusion.88
  135.3 1.9 fusion.87
  137.2 1.8 convolution_bitcast_fusion.3
  139.0 1.8 fusion.88
  141.1 1.9 fusion.87
  142.9 1.8 convolution_bitcast_fusion.3
  144.8 1.8 fusion.88
  146.8 1.9 fusion.87
  148.7 1.8 convolution_bitcast_fusion.3
  150.5 1.8 fusion.88
  152.6 1.9 fusion.87
  154.4 1.8 convolution_bitcast_fusion.3
  156.3 1.8 fusion.88
  158.3 1.9 fusion.87
  160.2 1.8 convolution_bitcast_fusion.3
  162.0 1.8 fusion.88
  164.1 1.9 fusion.57
  166.1 1.8 convolution_bitcast_fusion.1
  168.9 2.0 %convolution_add_fusion = f32[512,512]{1,0:T(8,128)S(1)} fusion(f32[512,512]{1,0:T(8,128)S(1)} %bitcast.126, f32[512]{0:T(512)S(1)} %bitcast.135, f32[512]{0:T(512)S(1)} %bitcast.143, f32[512,512]{1,0:T(8,128)S(1)} %get-tuple-element.24, f32[]{:T(128)S(6)} %sqrt.3), kind=kOutput, calls=%fused_computation.17 | convolution fusion | flops 1611923456 | bytes 3149828 | tf_op jit(solution)/shard_map/ij,...iv->...jv/dot_general | solution.py:67
  170.9 1.6 reshape.279
  172.5 3.6 %all-to-all-start.2 = ((f32[8,64,2,1,256]{4,2,1,3,0:T(2,128)}), f32[8,64,2,1,256]{4,2,1,3,0:T(2,128)S(1)}, u32[]{:S(2)}, u32[]{:S(2)}) async-start(f32[8,64,2,1,256]{4,2,1,3,0:T(2,128)} %bitcast.42), calls=%async_computation.2 | async-start | bytes 2097152 | tf_op jit(solution)/shard_map/all_to_all | solution.py:156
  176.1 2.1 %reduce_sum.39 = f32[3,512]{1,0:T(4,128)S(1)} reduce(f32[3,1,1,512,512]{4,3,2,1,0:T(8,128)} %param.10, f32[]{:T(128)} %constant.20.clone.1), dimensions={1,2,3}, to_apply=%region_6.7 | reduce | flops 784896 | bytes 3151876 | tf_op jit(solution)/shard_map/reduce_sum | solution.py:66
  178.3 8.5 %add_bitcast_fusion = f32[3,1,1,512,512]{3,4,0,2,1:T(8,128)} fusion(f32[3,1,1,512,512]{4,3,2,1,0:T(8,128)} %param.10, f32[3,512]{1,0:T(4,128)S(1)} %broadcast_multiply_fusion, f32[512]{0:T(512)S(1)} %bitcast.136, f32[512,512]{1,0:T(8,128)S(1)} %get-tuple-element.24, f32[]{:T(128)S(6)} %sqrt.3), kind=kOutput, calls=%fused_computation.12 | convolution fusion | flops 4834197504 | bytes 7348228 | tf_op jit(solution)/shard_map/ij,...iv->...jv/dot_general | solution.py:67
  186.8 3.5 %copy.47 = f32[3,1,1,512,512]{4,3,2,1,0:T(8,128)} copy(f32[3,1,1,512,512]{3,4,0,2,1:T(8,128)} %add_bitcast_fusion) | data formatting | bytes 6291456
  (82 shorter events, 22.8 us)
Async XLA Ops:
  0.6 103.1 %copy-start = (f32[4096]{0:T(1024)S(1)}, f32[4096]{0:T(1024)}, u32[]{:S(2)}) copy-start(f32[4096]{0:T(1024)} %param.14) | copy-start | bytes 49156
  4.1 4.7 %copy-start.10 = (f32[2048]{0:T(1024)S(1)}, f32[2048]{0:T(1024)}, u32[]{:S(2)}) copy-start(f32[2048]{0:T(1024)} %param.11) | copy-start | bytes 24580
  4.1 4.7 %copy-start.9 = (s32[1,1,1024]{2,1,0:T(1,128)S(1)}, s32[1,1,1024]{2,1,0:T(1,128)}, u32[]{:S(2)}) copy-start(s32[1,1,1024]{2,1,0:T(1,128)} %param.15) | copy-start | bytes 12292
  4.1 13.9 %copy-start.1 = (s32[4096]{0:T(1024)S(1)}, s32[4096]{0:T(1024)}, u32[]{:S(2)}) copy-start(s32[4096]{0:T(1024)} %param.12) | copy-start | bytes 49156
  4.6 14.9 %collective-permute-start = (f32[64]{0:T(128)S(1)}, f32[64]{0:T(128)S(1)}, u32[]{:S(2)}, u32[]{:S(2)}) collective-permute-start(f32[64]{0:T(128)S(1)} %slice_bitcast_fusion.4), channel_id=1, source_target_pairs={{0,4},{4,8},{8,12},{12,0},{1,5},{5,9},{9,13},{13,1},{2,6},{6,10},{... | collective-permute-start | bytes 776 | tf_op jit(solution)/shard_map/ppermute | solution.py:21
  19.8 3.6 %collective-permute-start.1 = (f32[64]{0:T(128)S(1)}, f32[64]{0:T(128)S(1)}, u32[]{:S(2)}, u32[]{:S(2)}) collective-permute-start(f32[64]{0:T(128)S(1)} %slice_bitcast_fusion.3), channel_id=1, source_target_pairs={{0,12},{4,0},{8,4},{12,8},{1,13},{5,1},{9,5},{13,9},{2,14},{6,2},{... | collective-permute-start | bytes 776 | tf_op jit(solution)/shard_map/ppermute | solution.py:21
  23.7 5.6 %collective-permute-start.2 = (f32[64]{0:T(128)S(1)}, f32[64]{0:T(128)S(1)}, u32[]{:S(2)}, u32[]{:S(2)}) collective-permute-start(f32[64]{0:T(128)S(1)} %slice_bitcast_fusion.2), channel_id=1, source_target_pairs={{0,4},{4,8},{8,12},{12,0},{1,5},{5,9},{9,13},{13,1},{2,6},{6,10},{... | collective-permute-start | bytes 776 | tf_op jit(solution)/shard_map/ppermute | solution.py:21
  29.7 9.1 %collective-permute-start.3 = (f32[64]{0:T(128)S(1)}, f32[64]{0:T(128)S(1)}, u32[]{:S(2)}, u32[]{:S(2)}) collective-permute-start(f32[64]{0:T(128)S(1)} %slice_bitcast_fusion.1), channel_id=1, source_target_pairs={{0,12},{4,0},{8,4},{12,8},{1,13},{5,1},{9,5},{13,9},{2,14},{6,2},{... | collective-permute-start | bytes 776 | tf_op jit(solution)/shard_map/ppermute | solution.py:21
  36.8 23.1 %collective-permute-start.5 = (f32[1024,64]{1,0:T(8,128)}, f32[1024,64]{1,0:T(8,128)}, u32[]{:S(2)}, u32[]{:S(2)}) collective-permute-start(f32[1024,64]{1,0:T(8,128)} %gather_fusion), channel_id=1, source_target_pairs={{4,0},{8,4},{12,8},{0,12},{5,1},{9,5},{13,9},{1,13},{6,2},{10,6},{... | collective-permute-start | bytes 786440 | tf_op jit(solution)/shard_map/ppermute | solution.py:33
  36.8 23.1 %collective-permute-start.4 = (f32[1024,64]{1,0:T(8,128)}, f32[1024,64]{1,0:T(8,128)}, u32[]{:S(2)}, u32[]{:S(2)}) collective-permute-start(f32[1024,64]{1,0:T(8,128)} %gather_fusion), channel_id=1, source_target_pairs={{0,4},{4,8},{8,12},{12,0},{1,5},{5,9},{9,13},{13,1},{2,6},{6,10},{... | collective-permute-start | bytes 786440 | tf_op jit(solution)/shard_map/ppermute | solution.py:30
  44.7 15.3 %copy-start.7 = (f32[1024,64]{1,0:T(8,128)S(1)}, f32[1024,64]{1,0:T(8,128)}, u32[]{:S(2)}) copy-start(f32[1024,64]{1,0:T(8,128)} %gather_fusion) | copy-start | bytes 786436
  46.6 46.2 %all-to-all-start = ((f32[1,64,2,8,256]{4,2,1,0,3:T(2,128)}), f32[1,64,2,8,256]{4,2,1,0,3:T(2,128)S(1)}, u32[]{:S(2)}, u32[]{:S(2)}) async-start(f32[1,64,2,8,256]{4,2,1,0,3:T(2,128)} %pad_maximum_fusion.1), calls=%async_computation | async-start | bytes 2097152 | tf_op jit(solution)/shard_map/all_to_all | solution.py:125
  92.8 1.0 copy-start.5
  93.8 29.2 %all-to-all-start.1 = ((f32[8,1024,64]{1,2,0:T(8,128)}), f32[8,1024,64]{1,2,0:T(8,128)S(1)}, u32[]{:S(2)}, u32[]{:S(2)}) async-start(f32[8,1024,64]{1,2,0:T(8,128)} %copy.41), calls=%async_computation.1 | async-start | bytes 4194304 | tf_op jit(solution)/shard_map/all_to_all | solution.py:140
  103.8 6.2 %copy-start.2 = (f32[4096]{0:T(1024)S(1)}, f32[4096]{0:T(1024)}, u32[]{:S(2)}) copy-start(f32[4096]{0:T(1024)} %param.13) | copy-start | bytes 49156
  118.8 2.4 %copy-start.6 = (f32[1,64,2,8,256]{4,2,1,0,3:T(2,128)S(1)}, f32[1,64,2,8,256]{4,2,1,0,3:T(2,128)}, u32[]{:S(2)}) copy-start(f32[1,64,2,8,256]{4,2,1,0,3:T(2,128)} %copy-done.5) | copy-start | bytes 3145732
  123.7 3.6 %copy-start.3 = (f32[8,1,1024,64]{2,3,0,1:T(8,128)}, f32[8,1,1024,64]{2,3,0,1:T(8,128)S(1)}, u32[]{:S(2)}) copy-start(f32[8,1,1024,64]{2,3,0,1:T(8,128)S(1)} %get-tuple-element.60) | copy-start | bytes 6291460
  164.1 1.9 copy-start.4
  166.0 2.9 %copy-start.8 = (f32[64,8,2,256]{3,1,2,0:T(8,128)S(1)}, f32[64,8,2,256]{3,1,2,0:T(8,128)}, u32[]{:S(2)}) copy-start(f32[64,8,2,256]{3,1,2,0:T(8,128)} %copy.54) | copy-start | bytes 3145732
  172.5 18.0 %all-to-all-start.2 = ((f32[8,64,2,1,256]{4,2,1,3,0:T(2,128)}), f32[8,64,2,1,256]{4,2,1,3,0:T(2,128)S(1)}, u32[]{:S(2)}, u32[]{:S(2)}) async-start(f32[8,64,2,1,256]{4,2,1,3,0:T(2,128)} %bitcast.42), calls=%async_computation.2 | async-start | bytes 2097152 | tf_op jit(solution)/shard_map/all_to_all | solution.py:156
where the time goes:
time: 193 us
  local copies, waits for them, and re-layouts  78.8 us (41%)
  matrix products  52.2 us (27%)
  starting transfers between devices  22 us (11%)
  waiting for transfers between devices  14.2 us (7%)
  other arithmetic  14.1 us (7%)
  blocking collectives  9.12 us (5%)
    gather x1, local copies, waits for them, and re-layouts, per_device(): picked = jnp.take(nearby, relative.reshape(-1), axis=0, mode='clip')  27.8 us
    unnamed x30, local copies, waits for them, and re-layouts  12.6 us
    dot_general x6, matrix products, newton_step(): middle = 1.5 * identity - 0.5 * jnp.dot(root_inv, approx, precision=highest)  11.2 us
    dot_general x6, matrix products, newton_step(): jnp.dot(approx, middle, precision=highest)  11.1 us
    dot_general x6, matrix products, newton_step(): jnp.dot(middle, root_inv, precision=highest)  11.1 us
    dot_general x2, matrix products, apply_transform(): jnp.einsum('ij,...iv->...jv', transform, states - state_mean, precision=h...  10.6 us
    ppermute x1, waiting for transfers between devices, with_halo(): lax.ppermute(lax.slice_in_dim(block, 0, width, axis=dim), axis, backward)  9.63 us
    all_gather x1, blocking collectives, per_device(): row_lists = lax.all_gather(tile_obs, ('grp', 'mem'), axis=1, tiled=True)[0]  9.12 us
  transfers between devices with their start and end apart: 9, of which 5 were waited for; matrix products, arithmetic and copies ran while one was open for 46% of the time, Pallas kernels for 0%

commit v1 on v0

v1 whole, which is shorter than its diff:
```python
import functools
import math

import jax
import jax.numpy as jnp
from jax import lax
from jax.experimental import pallas as pl
from jax.experimental.pallas import tpu as pltpu
from jax.sharding import PartitionSpec as P

OBS_DEV = 1024
ITERS = 6
MODEL_STEPS = 2
LOC = 512
EDGE = 128
UNROLL = 32

flux_scale = 0.9
wave_scale = 0.9
f32 = jnp.float32
bf16 = jnp.bfloat16

VMEM = pl.BlockSpec(memory_space=pltpu.VMEM)
SMEM = pl.BlockSpec(memory_space=pltpu.SMEM)


def params():
    return pltpu.CompilerParams(vmem_limit_bytes=56 * 1024 * 1024)


def cost(flops, moved):
    return pl.CostEstimate(flops=flops, bytes_accessed=moved, transcendentals=0)


def split(x):
    high = x.astype(bf16)
    return high, (x - high.astype(f32)).astype(bf16)


def dot(a, b):
    return jnp.dot(a, b, preferred_element_type=f32)


def product(a, b):
    return dot(a[0], b[0]) + (dot(a[0], b[1]) + dot(a[1], b[0]))


def shifted(array, axis, by):
    peers = lax.axis_size(axis)
    return lax.ppermute(array, axis, [(i, (i + by) % peers) for i in range(peers)])


def copy_rows(index_ref, table_ref, out_ref, count):
    def body(step, carry):
        base = pl.multiple_of(step * UNROLL, UNROLL)
        rows = [table_ref[pl.ds(index_ref[base + j], 1), :] for j in range(UNROLL)]
        for j in range(UNROLL):
            out_ref[pl.ds(base + j, 1), :] = rows[j]
        return carry

    lax.fori_loop(0, count // UNROLL, body, 0)


def paired(low, high):
    lane = lax.broadcasted_iota(jnp.int32, low.shape, low.ndim - 1)
    return jnp.where(lane < low.shape[-1] // 2, low, high)


def forecast_kernel(
    index_ref, state_ref, left_ref, right_ref, depth_ref, fields_ref, picked_ref, table, rows
):
    members, _, cells = state_ref.shape
    parts = fields_ref.shape[0]
    width = cells // parts
    total = cells + 2 * EDGE
    h = jnp.concatenate([left_ref[:, 0, :], state_ref[:, 0, :], right_ref[:, 0, :]], axis=1)
    u = jnp.concatenate([left_ref[:, 1, :], state_ref[:, 1, :], right_ref[:, 1, :]], axis=1)
    depth = flux_scale * depth_ref[...]
    for repeat in range(MODEL_STEPS):
        h = h - depth * (u - pltpu.roll(u, 1, 1))
        u = u - wave_scale * (pltpu.roll(h, total - 1, 1) - h)
    for part in range(parts):
        fields_ref[part, 0] = h[:, EDGE + part * width : EDGE + (part + 1) * width]
        fields_ref[part, 1] = u[:, EDGE + part * width : EDGE + (part + 1) * width]
    own = h[:, EDGE : EDGE + cells]
    table[...] = jnp.concatenate([own, own], axis=0).T
    count = rows.shape[0]
    copy_rows(index_ref, table, rows, count)
    picked_ref[...] = paired(rows[: count // 2, :], rows[count // 2 :, :])


def listed_kernel(index_ref, before_ref, here_ref, after_ref, out_ref, table, rows):
    half = here_ref.shape[0]
    for place, block_ref in enumerate((before_ref, here_ref, after_ref)):
        block = block_ref[...]
        turned = pltpu.roll(block, block.shape[1] // 2, 1)
        table[2 * place * half : (2 * place + 1) * half, :] = paired(block, turned)
        table[(2 * place + 1) * half : (2 * place + 2) * half, :] = paired(turned, block)
    parts, slots_half, _ = out_ref.shape
    count = 2 * slots_half
    copy_rows(index_ref, table, rows, parts * count)
    for part in range(parts):
        out_ref[part] = paired(
            rows[part * count : part * count + slots_half, :],
            rows[part * count + slots_half : (part + 1) * count, :],
        )


def facts_kernel(index_ref, facts_ref, out_ref, table):
    table[...] = facts_ref[...].T
    copy_rows(index_ref, table, out_ref, out_ref.shape[0])


def transform_kernel(
    cell_total, center_ref, arrived_ref, facts_ref, high_ref, low_ref, spread, near, root
):
    parts, half, lanes = arrived_ref.shape
    block = lanes // 2
    members = parts * block
    for part in range(parts):
        spread[:half, part * block : (part + 1) * block] = arrived_ref[part, :, :block]
        spread[half:, part * block : (part + 1) * block] = arrived_ref[part, :, block:]
    level = facts_ref[:, 0:1]
    sigma = facts_ref[:, 1:2]
    distance = jnp.abs(facts_ref[:, 2:3] - center_ref[0])
    distance = jnp.minimum(distance, float(cell_total) - distance)
    weight = jnp.exp(-0.5 * (distance / LOC) ** 2) / (sigma * sigma)
    weight = jnp.where(facts_ref[:, 3:4] > 0.0, weight, jnp.zeros_like(weight))
    predicted = spread[...]
    mean = jnp.sum(predicted, axis=1, keepdims=True) / members
    deviation = predicted - mean
    innovation = jnp.sum(deviation * (weight * (level - mean)), axis=0, keepdims=True)
    scaled = split((deviation * jnp.sqrt(weight)).T)
    across = (((1,), (1,)), ((), ()))
    gram = lax.dot_general(scaled[0], scaled[0], across, preferred_element_type=f32)
    mixed = lax.dot_general(scaled[0], scaled[1], across, preferred_element_type=f32)
    gram = gram + (mixed + mixed.T)
    row = lax.broadcasted_iota(jnp.int32, (members, members), 0)
    column = lax.broadcasted_iota(jnp.int32, (members, members), 1)

    def middle(value):
        return jnp.where(row == column, 1.5, 0.0) - 0.5 * value

    matrix = gram + jnp.where(row == column, float(members - 1), 0.0)
    bound = jnp.max(jnp.sum(jnp.abs(matrix), axis=0, keepdims=True))
    start = matrix / bound
    first = middle(start)
    root[...] = first
    near[...] = product(split(start), split(first))

    def newton_step(repeat, carry):
        y = split(near[...])
        z = split(root[...])
        t = split(middle(product(z, y)))
        near[...] = product(y, t)
        root[...] = product(t, z)
        return carry

    lax.fori_loop(0, ITERS - 2, newton_step, 0)
    z = split(root[...])
    t = split(middle(product(z, split(near[...]))))
    cover_root = product(t, z) / jnp.sqrt(bound)
    once = jnp.sum(cover_root * innovation, axis=1, keepdims=True)
    mean_weight = jnp.sum(cover_root * once, axis=0, keepdims=True)
    high, low = split(math.sqrt(members - 1) * cover_root + mean_weight)
    high_ref[...] = high
    low_ref[...] = low


def moved(states, high, low):
    mean = jnp.sum(states, axis=0, keepdims=True) / states.shape[0]
    return mean + product((high, low), split(states - mean))


def apply_fields_kernel(high_ref, low_ref, fields_ref, out_ref):
    parts, variables, block, width = fields_ref.shape
    for variable in range(variables):
        states = fields_ref[:, variable].reshape(parts * block, width)
        result = moved(states, high_ref[...], low_ref[...])
        out_ref[:, variable] = result.reshape(parts, block, width)


def apply_lags_kernel(high_ref, low_ref, lag_ref, out_ref):
    out_ref[0] = moved(lag_ref[0], high_ref[...], low_ref[...])


def per_device(
    current_state, lagged_states, water_depth, obs_cells, obs_values, obs_errors, tile_obs
):
    block = current_state.shape[0]
    cells = current_state.shape[2]
    parts = lax.axis_size("grp") * lax.axis_size("mem")
    tile_count = lax.axis_size("tile")
    tile_index = lax.axis_index("tile")
    part_index = lax.axis_index("grp") * lax.axis_size("mem") + lax.axis_index("mem")
    obs_total = obs_values.shape[0]
    width = cells // parts
    members = block * parts
    slots = tile_obs.shape[-1]
    group = ("grp", "mem")

    left = shifted(current_state[:, :, cells - EDGE :], "tile", 1)
    right = shifted(current_state[:, :, :EDGE], "tile", -1)
    depth_left = shifted(water_depth[cells - EDGE :], "tile", 1)
    depth_right = shifted(water_depth[:EDGE], "tile", -1)
    depth = jnp.concatenate([depth_left, water_depth, depth_right])[None]

    own_list = tile_obs[0, 0]
    relative = (jnp.maximum(own_list, 0) - (tile_index - 1) * OBS_DEV) % obs_total
    relative = jnp.where(own_list >= 0, relative, 0)
    relative = jnp.clip(relative, 0, 3 * OBS_DEV - 1)
    all_lists = lax.all_gather(relative, group, axis=0, tiled=True)
    local_cells = lax.dynamic_slice_in_dim(obs_cells, tile_index * OBS_DEV, OBS_DEV)
    local_cells = jnp.clip(local_cells - tile_index * cells, 0, cells - 1)

    def around(array):
        return jnp.concatenate(
            [
                lax.dynamic_slice_in_dim(
                    array, (tile_index + by) % tile_count * OBS_DEV, OBS_DEV
                )
                for by in (-1, 0, 1)
            ]
        )

    nothing = jnp.zeros((3 * OBS_DEV,), f32)
    facts_table = jnp.stack(
        [around(obs_values), around(obs_errors), around(obs_cells).astype(f32)] + [nothing] * 5
    )
    facts_rows = pl.pallas_call(
        facts_kernel,
        out_shape=jax.ShapeDtypeStruct((slots, 8), f32),
        in_specs=[SMEM, VMEM],
        out_specs=VMEM,
        scratch_shapes=[pltpu.VMEM((3 * OBS_DEV, 8), f32)],
        compiler_params=params(),
        cost_estimate=cost(0, 4 << 20),
        name="facts",
    )(relative, facts_table)
    usable = (own_list >= 0).astype(f32)
    facts = jnp.concatenate([facts_rows[:, :3], usable[:, None], facts_rows[:, 4:]], axis=1)

    fields, picked = pl.pallas_call(
        forecast_kernel,
        out_shape=(
            jax.ShapeDtypeStruct((parts, 2, block, width), f32),
            jax.ShapeDtypeStruct((OBS_DEV // 2, 2 * block), f32),
        ),
        in_specs=[SMEM] + [VMEM] * 4,
        out_specs=(VMEM, VMEM),
        scratch_shapes=[
            pltpu.VMEM((cells, 2 * block), f32),
            pltpu.VMEM((OBS_DEV, 2 * block), f32),
        ],
        compiler_params=params(),
        cost_estimate=cost(0, 8 << 20),
        name="forecast",
    )(local_cells, current_state, left, right, depth)

    before = shifted(picked, "tile", 1)
    after = shifted(picked, "tile", -1)
    regrouped = lax.all_to_all(fields, group, split_axis=0, concat_axis=0, tiled=True)

    listed = pl.pallas_call(
        listed_kernel,
        out_shape=jax.ShapeDtypeStruct((parts, slots // 2, 2 * block), f32),
        in_specs=[SMEM] + [VMEM] * 3,
        out_specs=VMEM,
        scratch_shapes=[
            pltpu.VMEM((3 * OBS_DEV, 2 * block), f32),
            pltpu.VMEM((parts * slots, 2 * block), f32),
        ],
        compiler_params=params(),
        cost_estimate=cost(0, 24 << 20),
        name="listed",
    )(all_lists, before, picked, after)
    arrived = lax.all_to_all(listed, group, split_axis=0, concat_axis=0, tiled=True)

    center = tile_index * cells + part_index * width + width // 2
    high, low = pl.pallas_call(
        functools.partial(transform_kernel, cells * tile_count),
        out_shape=(jax.ShapeDtypeStruct((members, members), bf16),) * 2,
        in_specs=[SMEM, VMEM, VMEM],
        out_specs=(VMEM, VMEM),
        scratch_shapes=[
            pltpu.VMEM((slots, members), f32),
            pltpu.VMEM((members, members), f32),
            pltpu.VMEM((members, members), f32),
        ],
        compiler_params=params(),
        cost_estimate=cost(2 * 51 * members**3, 8 << 20),
        name="transform",
    )(center.astype(f32)[None], arrived, facts)

    analysed = pl.pallas_call(
        apply_fields_kernel,
        out_shape=jax.ShapeDtypeStruct(fields.shape, f32),
        in_specs=[VMEM] * 3,
        out_specs=VMEM,
        compiler_params=params(),
        cost_estimate=cost(2 * 3 * members**3, 4 << 20),
        name="apply_fields",
    )(high, low, regrouped)
    returned = lax.all_to_all(analysed, group, split_axis=0, concat_axis=0, tiled=True)

    lags = lagged_states.shape[0]
    unknowns = lagged_states.shape[-1]
    whole = pl.BlockSpec((members, members), lambda i: (0, 0))
    one = pl.BlockSpec((1, members, unknowns), lambda i: (i, 0, 0))
    older = pl.pallas_call(
        apply_lags_kernel,
        grid=(lags,),
        out_shape=jax.ShapeDtypeStruct((lags, members, unknowns), f32),
        in_specs=[whole, whole, one],
        out_specs=one,
        compiler_params=params(),
        cost_estimate=cost(2 * 9 * members**3, 16 << 20),
        name="apply_lags",
    )(high, low, lagged_states[:, 0, 0])
    analysis_state = returned.transpose(2, 1, 0, 3).reshape(block, 2, cells)
    return (analysis_state, older[:, None, None])


def solution(mesh):
    placed = (
        P(("grp", "mem"), None, "tile"),
        P(None, "tile", ("grp", "mem"), None, None),
        P("tile"),
        P(),
        P(),
        P(),
        P("tile", ("grp", "mem"), None),
    )
    return jax.shard_map(
        per_device,
        mesh=mesh,
        in_specs=placed,
        out_specs=(P(("grp", "mem"), None, "tile"), P(None, "tile", ("grp", "mem"), None, None)),
        check_vma=False,
    )
```

time: 193 us -> 127 us (0.66)
  local copies, waits for them, and re-layouts: 78.8 us -> 9.64 us
  matrix products: 52.2 us -> 0 us
  Pallas kernels: 0 us -> 48.1 us
  waiting for transfers between devices: 14.2 us -> 29.4 us
  other arithmetic: 14.1 us -> 5.7 us
    dot_general x24 -> x0, matrix products: 52.2 us -> none  [the longest x6 11.2 us: newton_step(): middle = 1.5 * identity - 0.5 * jnp.dot(root_inv, approx, precision=highest)]
    gather x5 -> x0, local copies, waits for them, and re-layouts: 50.2 us -> none  [the longest x1 27.8 us: per_device(): picked = jnp.take(nearby, relative.reshape(-1), axis=0, mode='clip')]
    pallas_call x0 -> x6, Pallas kernels: none -> 48.1 us  [the longest x1 19.9 us: per_device(): pl.pallas_call(functools.partial(transform_kernel, cells * tile_count), o...]
    all_to_all x3, waiting for transfers between devices: 1.45 us -> 26.2 us  [the longest x1 18 us: per_device(): lax.all_to_all(listed, group, split_axis=0, concat_axis=0, tiled=True)]
    ppermute x2 -> x0, waiting for transfers between devices: 9.63 us -> none  [the longest x1 9.63 us: with_halo(): lax.ppermute(lax.slice_in_dim(block, 0, width, axis=dim), axis, backward)]
    unnamed x30 -> x20, local copies, waits for them, and re-layouts: 12.6 us -> 5.23 us
    reshape x2 -> x0, local copies, waits for them, and re-layouts: 5.4 us -> none  [the longest x1 3.78 us: per_device(): picked = picked.reshape(trial_bundles, rows_here.shape[0], trial_slab_lines)]
    concatenate x4 -> x0, local copies, waits for them, and re-layouts: 4.39 us -> none  [the longest x2 2.22 us: advance(): jnp.concatenate([velocity_left[:, None], fluid_speed[:, :-1]], axis=1)]
  transfers between devices with their start and end apart: 9 -> 9, of which waited for: 5 -> 3; matrix products, arithmetic and copies ran while one was open for 46% -> 7% of each run, Pallas kernels for 0% -> 23%
where the time goes in v1:
time: 127 us; the launch traced here: 126 us
  Pallas kernels  48.1 us (38%)
  waiting for transfers between devices  29.4 us (23%)
  starting transfers between devices  22.3 us (18%)
  blocking collectives  10.1 us (8%)
  local copies, waits for them, and re-layouts  9.64 us (8%)
  other arithmetic  5.7 us (4%)
    pallas_call x1, Pallas kernels, per_device(): pl.pallas_call(functools.partial(transform_kernel, cells * tile_count), o...  19.9 us
    all_to_all x1, waiting for transfers between devices, per_device(): lax.all_to_all(listed, group, split_axis=0, concat_axis=0, tiled=True)  18 us
    ppermute x6, starting transfers between devices, shifted(): lax.ppermute(array, axis, [(i, (i + by) % peers) for i in range(peers)])  11 us
    pallas_call x1, Pallas kernels, per_device(): pl.pallas_call(listed_kernel, out_shape=jax.ShapeDtypeStruct((parts, slot...  10.8 us
    all_gather x1, blocking collectives, per_device(): all_lists = lax.all_gather(relative, group, axis=0, tiled=True)  10.1 us
    all_to_all x1, waiting for transfers between devices, per_device(): lax.all_to_all(analysed, group, split_axis=0, concat_axis=0, tiled=True)  8.2 us
    pallas_call x1, Pallas kernels, per_device(): pl.pallas_call(apply_lags_kernel, grid=(lags,), out_shape=jax.ShapeDtypeS...  6.27 us
    unnamed x20, local copies, waits for them, and re-layouts  5.23 us
  transfers between devices with their start and end apart: 9, of which 3 were waited for; matrix products, arithmetic and copies ran while one was open for 7% of the time, Pallas kernels for 23%

profile of v1, /device:TPU:0, one launch (start us, length us, event | category | flops | bytes accessed | tf_op | source)
XLA Modules:
  0.0 126.1 jit_solution(11669066287100299599)
XLA Ops:
  0.6 0.9 fusion.4
  1.5 3.1 %collective-permute-start = (f32[64,2,128]{2,1,0:T(2,128)S(1)}, f32[64,2,128]{2,1,0:T(2,128)S(1)}, u32[]{:S(2)}, u32[]{:S(2)}) collective-permute-start(f32[64,2,128]{2,1,0:T(2,128)S(1)} %get-tuple-element.19), channel_id=1, source_target_pairs={{0,4},{4,8},{8,12},{12,0},{1,5},{5,9},{9,13},{13,1},{2,6},{6,10},{... | collective-permute-start | bytes 196616 | tf_op jit(solution)/shard_map/ppermute | solution.py:50
  4.6 2.1 %collective-permute-start.1 = (f32[64,2,128]{2,1,0:T(2,128)S(1)}, f32[64,2,128]{2,1,0:T(2,128)S(1)}, u32[]{:S(2)}, u32[]{:S(2)}) collective-permute-start(f32[64,2,128]{2,1,0:T(2,128)S(1)} %get-tuple-element.18), channel_id=1, source_target_pairs={{0,12},{4,0},{8,4},{12,8},{1,13},{5,1},{9,5},{13,9},{2,14},{6,2},{... | collective-permute-start | bytes 196616 | tf_op jit(solution)/shard_map/ppermute | solution.py:50
  6.7 0.7 fusion.8
  7.4 2.0 %collective-permute-start.3 = (f32[128]{0:T(128)S(1)}, f32[128]{0:T(128)S(1)}, u32[]{:S(2)}, u32[]{:S(2)}) collective-permute-start(f32[128]{0:T(128)S(1)} %get-tuple-element.31), channel_id=1, source_target_pairs={{0,12},{4,0},{8,4},{12,8},{1,13},{5,1},{9,5},{13,9},{2,14},{6,2},{... | collective-permute-start | bytes 1544 | tf_op jit(solution)/shard_map/ppermute | solution.py:50
  9.4 0.1 collective-permute-start.2
  9.4 0.7 fusion.3
  10.2 1.4 %fusion.5 = (s32[1024]{0:T(1024)S(1)}, s32[1024]{0:T(1024)}, s32[1024]{0:T(1024)S(1)}, s32[1024]{0:T(1024)S(1)}) fusion(s32[4096]{0:T(1024)} %param.10, s32[]{:T(128)S(6)} %select_n.59, s32[]{:T(128)S(6)} %mul.31, s32[]{:T(128)S(6)} %select_n.57, s32[]{:T(128)S(6)} %select_n.63, s32[]{:T(128)S(6)} %select_n.61), kind=kLoop, calls=%fused_computation.17 | loop fusion | flops 2048 | bytes 32788 | tf_op jit(solution)/shard_map/dynamic_slice | solution.py:219
  11.5 0.0 collective-permute-done.3
  11.5 3.2 %collective-permute-done.2 = f32[128]{0:T(128)S(1)} collective-permute-done((f32[128]{0:T(128)S(1)}, f32[128]{0:T(128)S(1)}, u32[]{:S(2)}, u32[]{:S(2)}) %collective-permute-start.2) | collective-permute-done | bytes 544 | tf_op jit(solution)/shard_map/ppermute | solution.py:50
  14.8 0.7 pad_maximum_fusion.1
  15.5 0.6 broadcast_in_dim.13.depth_ref
  16.0 0.0 collective-permute-done.left_ref
  16.1 0.0 collective-permute-done.1.right_ref
  16.1 0.0 copy-start.5
  16.1 0.6 copy-done.4
  16.7 0.0 copy-done.5
  16.7 4.4 %forecast.1 = (f32[8,2,64,256]{3,2,1,0:T(8,128)}, f32[512,128]{1,0:T(8,128)}) custom-call(s32[1024]{0:T(1024)} %get-tuple-element.21.index_ref, f32[64,2,2048]{2,1,0:T(2,128)} %state_ref.1, f32[64,2,128]{2,1,0:T(2,128)} %copy-done.4, f32[64,2,128]{2,1,0:T(2,128)} %copy-done.5, f32[1,2304]{1,0:T(1,128)} %broadcast_in_dim.13.depth_ref), custom_call_target="tpu_custom_call" | custom-call | bytes 8388608 | tf_op jit(solution)/shard_map/forecast/pallas_call | solution.py:243
  21.1 0.0 collective-permute-start.4
  21.1 3.8 %collective-permute-start.5 = (f32[512,128]{1,0:T(8,128)}, f32[512,128]{1,0:T(8,128)S(1)}, u32[]{:S(2)}, u32[]{:S(2)}) collective-permute-start(f32[512,128]{1,0:T(8,128)} %get-tuple-element.6.here_ref), channel_id=1, source_target_pairs={{0,12},{4,0},{8,4},{12,8},{1,13},{5,1},{9,5},{13,9},{2,14},{6,2},{... | collective-permute-start | bytes 786440 | tf_op jit(solution)/shard_map/ppermute | solution.py:50
  24.9 0.7 maximum_subtract_fusion
  25.6 10.1 %all_gather.3.index_ref = s32[8192]{0:T(1024)} all-gather(s32[1024]{0:T(1024)S(1)} %fusion.2.index_ref), channel_id=1, replica_groups=mesh['grp'=2,'tile'=4,'mem'=4] {'grp','mem'}, dimensions={0}, use_global_device_ids=true | all-gather | bytes 36864 | tf_op jit(solution)/shard_map/all_gather | solution.py:212
  35.8 0.0 collective-permute-done.4.before_ref
  35.8 0.0 collective-permute-done.5.after_ref
  35.8 0.7 copy-done.2
  36.5 0.7 copy-done.3
  37.2 10.8 %listed.1 = f32[8,512,128]{2,1,0:T(8,128)} custom-call(s32[8192]{0:T(1024)} %all_gather.3.index_ref, f32[512,128]{1,0:T(8,128)} %copy-done.2, f32[512,128]{1,0:T(8,128)} %get-tuple-element.6.here_ref, f32[512,128]{1,0:T(8,128)} %copy-done.3), custom_call_target="tpu_custom_call" | custom-call | bytes 25165824 | tf_op jit(solution)/shard_map/listed/pallas_call | solution.py:264
  48.0 0.0 copy-done.6
  48.0 3.6 %all-to-all-start = ((f32[8,512,128]{2,1,0:T(8,128)}), f32[8,512,128]{2,1,0:T(8,128)S(1)}, u32[]{:S(2)}, u32[]{:S(2)}) async-start(f32[8,512,128]{2,1,0:T(8,128)} %listed.1), calls=%async_computation | async-start | bytes 4194304 | tf_op jit(solution)/shard_map/all_to_all | solution.py:277
  51.6 0.0 copy-done.7
  51.6 0.0 copy-done.8
  51.7 0.7 stack.16.facts_ref
  52.4 3.1 %facts.1 = f32[1024,8]{1,0:T(8,128)} custom-call(s32[1024]{0:T(1024)} %copy-done.6, f32[8,3072]{1,0:T(8,128)} %stack.16.facts_ref), custom_call_target="tpu_custom_call" | custom-call | bytes 4194304 | tf_op jit(solution)/shard_map/facts/pallas_call | solution.py:230
  55.6 1.2 slice.25
  56.8 0.2 copy.20
  57.0 2.2 %pad_maximum_fusion.facts_ref = f32[1024,8]{1,0:T(8,128)} fusion(f32[1024,4]{1,0:T(8,128)S(1)} %slice.25, f32[1024,1]{1,0:T(8,128)S(1)} %copy.20, f32[1024,3]{1,0:T(8,128)} %bitcast.17), kind=kLoop, calls=%fused_computation | loop fusion | flops 16384 | bytes 65536 | tf_op jit(solution)/shard_map/concatenate | solution.py:241
  59.2 18.0 %all-to-all-done.arrived_ref = f32[8,512,128]{2,1,0:T(8,128)S(1)} async-done(((f32[8,512,128]{2,1,0:T(8,128)}), f32[8,512,128]{2,1,0:T(8,128)S(1)}, u32[]{:S(2)}, u32[]{:S(2)}) %all-to-all-start) | async-done | bytes 2097184 | tf_op jit(solution)/shard_map/all_to_all | solution.py:277
  77.2 3.7 %all-to-all-start.1 = ((f32[8,2,64,256]{3,2,1,0:T(8,128)}), f32[8,2,64,256]{3,2,1,0:T(8,128)S(1)}, u32[]{:S(2)}, u32[]{:S(2)}) async-start(f32[8,2,64,256]{3,2,1,0:T(8,128)} %get-tuple-element.9), calls=%async_computation.1 | async-start | bytes 2097152 | tf_op jit(solution)/shard_map/all_to_all | solution.py:262
  81.0 0.0 copy-done.1
  81.0 19.9 %transform.1 = (bf16[512,512]{1,0:T(8,128)(2,1)}, bf16[512,512]{1,0:T(8,128)(2,1)}) custom-call(f32[1]{0:T(128)} %bitcast.center_ref, f32[8,512,128]{2,1,0:T(8,128)} %copy-done.1, f32[1024,8]{1,0:T(8,128)} %pad_maximum_fusion.facts_ref), custom_call_target="tpu_custom_call" | custom-call | flops 13690208256 | bytes 8388608 | tf_op jit(solution)/shard_map/transform/pallas_call | solution.py:280
  100.9 0.0 all-to-all-done.1.fields_ref
  100.9 1.0 copy-done
  101.8 3.6 %apply_fields.1 = f32[8,2,64,256]{3,2,1,0:T(8,128)} custom-call(bf16[512,512]{1,0:T(8,128)(2,1)} %get-tuple-element.7.high_ref, bf16[512,512]{1,0:T(8,128)(2,1)} %get-tuple-element.8.low_ref, f32[8,2,64,256]{3,2,1,0:T(8,128)} %copy-done), custom_call_target="tpu_custom_call" | custom-call | flops 805306368 | bytes 4194304 | tf_op jit(solution)/shard_map/apply_fields/pallas_call | solution.py:295
  105.5 3.9 %all-to-all-start.2 = ((f32[8,2,64,256]{3,2,1,0:T(8,128)}), f32[8,2,64,256]{3,2,1,0:T(8,128)S(1)}, u32[]{:S(2)}, u32[]{:S(2)}) async-start(f32[8,2,64,256]{3,2,1,0:T(8,128)} %apply_fields.1), calls=%async_computation.2 | async-start | bytes 2097152 | tf_op jit(solution)/shard_map/all_to_all | solution.py:304
  109.4 6.3 %apply_lags.1 = f32[3,512,512]{2,1,0:T(8,128)} custom-call(bf16[512,512]{1,0:T(8,128)(2,1)} %get-tuple-element.7.high_ref, bf16[512,512]{1,0:T(8,128)(2,1)} %get-tuple-element.8.low_ref, f32[3,512,512]{2,1,0:T(8,128)} %bitcast.25), custom_call_target="tpu_custom_call" | custom-call | flops 2415919104 | bytes 16777216 | tf_op jit(solution)/shard_map/apply_lags/pallas_call | solution.py:310
  115.7 8.2 %all-to-all-done.2 = f32[8,2,64,256]{3,2,1,0:T(8,128)S(1)} async-done(((f32[8,2,64,256]{3,2,1,0:T(8,128)}), f32[8,2,64,256]{3,2,1,0:T(8,128)S(1)}, u32[]{:S(2)}, u32[]{:S(2)}) %all-to-all-start.2) | async-done | bytes 1048608 | tf_op jit(solution)/shard_map/all_to_all | solution.py:304
  123.9 0.6 copy.24
  124.5 1.6 %reshape.74 = f32[64,2,2048]{2,1,0:T(2,128)} reshape(f32[64,2,8,256]{3,2,1,0:T(8,128)S(1)} %copy.24) | data formatting | bytes 2097152
  (15 shorter events, 0.1 us)
Async XLA Ops:
  1.5 14.5 %collective-permute-start = (f32[64,2,128]{2,1,0:T(2,128)S(1)}, f32[64,2,128]{2,1,0:T(2,128)S(1)}, u32[]{:S(2)}, u32[]{:S(2)}) collective-permute-start(f32[64,2,128]{2,1,0:T(2,128)S(1)} %get-tuple-element.19), channel_id=1, source_target_pairs={{0,4},{4,8},{8,12},{12,0},{1,5},{5,9},{9,13},{13,1},{2,6},{6,10},{... | collective-permute-start | bytes 196616 | tf_op jit(solution)/shard_map/ppermute | solution.py:50
  4.6 11.4 %collective-permute-start.1 = (f32[64,2,128]{2,1,0:T(2,128)S(1)}, f32[64,2,128]{2,1,0:T(2,128)S(1)}, u32[]{:S(2)}, u32[]{:S(2)}) collective-permute-start(f32[64,2,128]{2,1,0:T(2,128)S(1)} %get-tuple-element.18), channel_id=1, source_target_pairs={{0,12},{4,0},{8,4},{12,8},{1,13},{5,1},{9,5},{13,9},{2,14},{6,2},{... | collective-permute-start | bytes 196616 | tf_op jit(solution)/shard_map/ppermute | solution.py:50
  7.4 4.1 %collective-permute-start.3 = (f32[128]{0:T(128)S(1)}, f32[128]{0:T(128)S(1)}, u32[]{:S(2)}, u32[]{:S(2)}) collective-permute-start(f32[128]{0:T(128)S(1)} %get-tuple-element.31), channel_id=1, source_target_pairs={{0,12},{4,0},{8,4},{12,8},{1,13},{5,1},{9,5},{13,9},{2,14},{6,2},{... | collective-permute-start | bytes 1544 | tf_op jit(solution)/shard_map/ppermute | solution.py:50
  9.4 5.4 %collective-permute-start.2 = (f32[128]{0:T(128)S(1)}, f32[128]{0:T(128)S(1)}, u32[]{:S(2)}, u32[]{:S(2)}) collective-permute-start(f32[128]{0:T(128)S(1)} %get-tuple-element.30), channel_id=1, source_target_pairs={{0,4},{4,8},{8,12},{12,0},{1,5},{5,9},{9,13},{13,1},{2,6},{6,10},{... | collective-permute-start | bytes 1544 | tf_op jit(solution)/shard_map/ppermute | solution.py:50
  16.0 0.6 copy-start.4
  16.1 0.6 copy-start.5
  21.1 14.7 %collective-permute-start.4 = (f32[512,128]{1,0:T(8,128)}, f32[512,128]{1,0:T(8,128)S(1)}, u32[]{:S(2)}, u32[]{:S(2)}) collective-permute-start(f32[512,128]{1,0:T(8,128)} %get-tuple-element.6.here_ref), channel_id=1, source_target_pairs={{0,4},{4,8},{8,12},{12,0},{1,5},{5,9},{9,13},{13,1},{2,6},{6,10},{... | collective-permute-start | bytes 786440 | tf_op jit(solution)/shard_map/ppermute | solution.py:50
  21.1 14.7 %collective-permute-start.5 = (f32[512,128]{1,0:T(8,128)}, f32[512,128]{1,0:T(8,128)S(1)}, u32[]{:S(2)}, u32[]{:S(2)}) collective-permute-start(f32[512,128]{1,0:T(8,128)} %get-tuple-element.6.here_ref), channel_id=1, source_target_pairs={{0,12},{4,0},{8,4},{12,8},{1,13},{5,1},{9,5},{13,9},{2,14},{6,2},{... | collective-permute-start | bytes 786440 | tf_op jit(solution)/shard_map/ppermute | solution.py:50
  25.6 22.3 %copy-start.6 = (s32[1024]{0:T(1024)}, s32[1024]{0:T(1024)S(1)}, u32[]{:S(2)}) copy-start(s32[1024]{0:T(1024)S(1)} %fusion.2.index_ref) | copy-start | bytes 12292
  35.7 15.8 %copy-start.7 = (f32[4096]{0:T(1024)S(1)}, f32[4096]{0:T(1024)}, u32[]{:S(2)}) copy-start(f32[4096]{0:T(1024)} %param.12) | copy-start | bytes 49156
  35.7 15.9 %copy-start.8 = (f32[4096]{0:T(1024)S(1)}, f32[4096]{0:T(1024)}, u32[]{:S(2)}) copy-start(f32[4096]{0:T(1024)} %param.11) | copy-start | bytes 49156
  35.8 0.7 copy-start.2
  36.5 0.7 copy-start.3
  48.0 29.2 %all-to-all-start = ((f32[8,512,128]{2,1,0:T(8,128)}), f32[8,512,128]{2,1,0:T(8,128)S(1)}, u32[]{:S(2)}, u32[]{:S(2)}) async-start(f32[8,512,128]{2,1,0:T(8,128)} %listed.1), calls=%async_computation | async-start | bytes 4194304 | tf_op jit(solution)/shard_map/all_to_all | solution.py:277
  77.2 3.8 %copy-start.1 = (f32[8,512,128]{2,1,0:T(8,128)}, f32[8,512,128]{2,1,0:T(8,128)S(1)}, u32[]{:S(2)}) copy-start(f32[8,512,128]{2,1,0:T(8,128)S(1)} %all-to-all-done.arrived_ref) | copy-start | bytes 6291460
  77.2 23.6 %all-to-all-start.1 = ((f32[8,2,64,256]{3,2,1,0:T(8,128)}), f32[8,2,64,256]{3,2,1,0:T(8,128)S(1)}, u32[]{:S(2)}, u32[]{:S(2)}) async-start(f32[8,2,64,256]{3,2,1,0:T(8,128)} %get-tuple-element.9), calls=%async_computation.1 | async-start | bytes 2097152 | tf_op jit(solution)/shard_map/all_to_all | solution.py:262
  100.9 1.0 copy-start
  105.5 18.4 %all-to-all-start.2 = ((f32[8,2,64,256]{3,2,1,0:T(8,128)}), f32[8,2,64,256]{3,2,1,0:T(8,128)S(1)}, u32[]{:S(2)}, u32[]{:S(2)}) async-start(f32[8,2,64,256]{3,2,1,0:T(8,128)} %apply_fields.1), calls=%async_computation.2 | async-start | bytes 2097152 | tf_op jit(solution)/shard_map/all_to_all | solution.py:304
